TPU v7x, 32 devices: a whole 2x2x4 slice. The times are simulated.
32 devices in a mesh: gx: 4 (over z), gy: 8 (over y, x, core).
Axes of the slice: x: 2, y: 2, z: 4, core: 2. Of those that a mesh axis runs over, the one named last changes fastest.
Arguments:
- features: bfloat16 [40960, 2048], P(('gx', 'gy')), may hold values from -6 to 6
- counts: int32 [32], P(('gx', 'gy')), may hold values from 128 to 1280, as said below
- ref_mean: float32 [2048], replicated, may hold values from -6 to 6
- ref_root: float32 [2048, 2048], P('gx', 'gy'), as said below
Outputs:
- mean: float32 [2048], replicated
- root: float32 [2048, 2048], P('gx', 'gy')
- distance: float32 [], replicated
Inputs may be any that keep to these rules, and one draw needn't show every extreme that they name: Entry b counts the valid rows of shard b, which come first in it; a multiple of 128; some shard is full in every draw. `ref_root`: symmetric and positive definite.
All inputs are finite; a program needn't handle non-finite values.
Results may differ from a plain program's by a relative error of at most 0.0015.
The roundings to bfloat16 on the way count: a program that leaves them out, or rounds other values in their place, can miss the bound.
Values may be sent and summed in bfloat16 or wider, within the bound.
A program may use at most 128 MiB of HBM per device.

v0:
```python
import jax
import jax.numpy as jnp
from jax import lax
from jax.sharding import PartitionSpec as P

ITERS = 4


def product(left, right):
    left_half = left.astype(jnp.bfloat16)
    right_half = right.astype(jnp.bfloat16)
    panel = lax.all_gather(left_half, "gy", axis=1, tiled=True)
    return jnp.dot(
        panel,
        lax.all_gather(right_half, "gx", axis=0, tiled=True),
        preferred_element_type=jnp.float32,
    )


def shards(features, counts, ref_mean, ref_root):
    width = features.shape[1]
    slots = features.shape[0]
    rows_x = lax.axis_size("gx")
    cols_y = lax.axis_size("gy")
    tile_rows = width // rows_x
    tile_cols = width // cols_y
    keep = (jnp.arange(slots, dtype=jnp.int32) < counts[0])[:, None]
    masked = jnp.where(keep, features, jnp.zeros_like(features))
    partial_gram = lax.dot_general(
        masked, features, (((0,), (0,)), ((), ())), preferred_element_type=jnp.float32
    )
    column_total = jnp.sum(masked.astype(jnp.float32), axis=0)
    local_count = counts[0].astype(jnp.float32)
    total, count = lax.psum((column_total, local_count), ("gx", "gy"))
    column_block = lax.psum_scatter(partial_gram, "gy", scatter_dimension=1, tiled=True)
    gram_tile = lax.psum_scatter(column_block, "gx", scatter_dimension=0, tiled=True)
    mean = total / count
    row_start = lax.axis_index("gx") * tile_rows
    col_start = lax.axis_index("gy") * tile_cols
    mean_rows = lax.dynamic_slice_in_dim(mean, row_start, tile_rows, 0)
    mean_cols = lax.dynamic_slice_in_dim(mean, col_start, tile_cols, 0)
    cov_tile = (gram_tile - count * mean_rows[:, None] * mean_cols[None, :]) / (count - 1.0)
    row_ids = jnp.arange(tile_rows, dtype=jnp.int32) + row_start
    col_ids = jnp.arange(tile_cols, dtype=jnp.int32) + col_start
    identity_tile = (row_ids[:, None] == col_ids[None, :]).astype(jnp.float32)
    half = product(cov_tile, ref_root)
    prod = product(ref_root, half)
    square_sum, cov_trace, root_square = lax.psum(
        (jnp.sum(prod * prod), jnp.sum(cov_tile * identity_tile), jnp.sum(ref_root * ref_root)),
        ("gx", "gy"),
    )
    scale = jnp.sqrt(square_sum + 1.0)
    current = prod / scale
    partner = identity_tile
    for step in range(ITERS):
        middle = 1.5 * identity_tile - 0.5 * product(partner, current)
        current, partner = (product(current, middle), product(middle, partner))
    last_trace = lax.psum(jnp.sum(current * identity_tile), ("gx", "gy"))
    root = jnp.sqrt(scale) * current
    distance = (
        jnp.sum((mean - ref_mean) ** 2)
        + cov_trace
        + root_square
        - 2.0 * jnp.sqrt(scale) * last_trace
    ) / 64.0
    return (mean, root, distance)


def solution(mesh):
    return jax.shard_map(
        shards,
        mesh=mesh,
        in_specs=(P(("gx", "gy"), None), P(("gx", "gy")), P(), P("gx", "gy")),
        out_specs=(P(), P("gx", "gy"), P()),
        check_vma=False,
    )
```

profile of v0, /device:TPU:0, one launch (start us, length us, event | category | flops | bytes accessed | tf_op | source)
XLA Modules:
  0.0 1031.6 jit_solution(1172393237996310174)
XLA Ops:
  7.9 18.1 %fusion = f32[2048,2048]{1,0:T(8,128)} fusion(bf16[1280,2048]{1,0:T(8,128)(2,1)} %param.4, pred[1280]{0:T(1024)(128)(4,1)S(1)} %iota_compare_fusion), kind=kOutput, calls=%fused_computation.1 | convolution fusion | flops 10740039680 | bytes 22021376 | tf_op jit(solution)/shard_map/dot_general | solution.py:29
  26.1 118.8 %reduce-scatter.3.cloned.1.call-done = f32[2048,256]{1,0:T(8,128)} async-done(((f32[2048,2048]{1,0:T(8,128)}), f32[2048,256]{1,0:T(8,128)}) %reduce-scatter.3.cloned.1.call-update) | async-done | bytes 2097168 | tf_op jit(solution)/shard_map/reduce_scatter | solution.py:35
  144.9 1.4 multiply_reduce_fusion
  146.4 3.6 convert_reduce_fusion
  150.0 42.2 %all-reduce.1 = (f32[2048]{0:T(1024)S(1)}, f32[]{:T(128)}) all-reduce(f32[2048]{0:T(1024)S(1)} %convert_reduce_fusion, f32[]{:T(128)S(6)} %convert_element_type.69), channel_id=1, replica_groups=mesh['gx'=4,'gy'=8] {'gx','gy'}, use_global_device_ids=true, to_apply=%region_1.2 | all-reduce | flops 2049 | bytes 16392 | tf_op jit(solution)/shard_map/psum | solution.py:34
  192.9 1.3 multiply_reduce_fusion.2
  194.2 0.1 dynamic_slice.7
  194.3 0.7 dynamic-slice_multiply_fusion
  195.0 1.9 fusion.16
  197.0 0.5 all-gather.33.cloned.1.call-update
  197.5 23.1 %all-gather.29.cloned.1.call-done = bf16[2048,256]{1,0:T(8,128)(2,1)} async-done(((bf16[512,256]{1,0:T(8,128)(2,1)}), bf16[2048,256]{1,0:T(8,128)(2,1)}) %all-gather.29.cloned.1.call-update) | async-done | bytes 1048592 | tf_op jit(solution)/shard_map/all_gather | solution.py:15
  220.6 29.8 %all-gather.27.cloned.1.call-done = bf16[512,2048]{1,0:T(8,128)(2,1)} async-done(((bf16[512,256]{1,0:T(8,128)(2,1)}), bf16[512,2048]{1,0:T(8,128)(2,1)}) %all-gather.27.cloned.1.call-update) | async-done | bytes 2097168 | tf_op jit(solution)/shard_map/all_gather | solution.py:12
  250.4 3.3 convolution_convert_fusion.6
  253.8 0.8 fusion.12
  254.7 0.0 all-gather.39.cloned.1.call-start
  254.7 25.6 %all-gather.33.cloned.1.call-done = bf16[512,2048]{1,0:T(8,128)(2,1)} async-done(((bf16[512,256]{1,0:T(8,128)(2,1)}), bf16[512,2048]{1,0:T(8,128)(2,1)}) %all-gather.33.cloned.1.call-update) | async-done | bytes 2097168 | tf_op jit(solution)/shard_map/all_gather | solution.py:12
  280.3 30.0 %all-gather.31.cloned.1.call-done = bf16[2048,256]{1,0:T(8,128)(2,1)} async-done(((bf16[512,256]{1,0:T(8,128)(2,1)}), bf16[2048,256]{1,0:T(8,128)(2,1)}) %all-gather.31.cloned.1.call-update) | async-done | bytes 1048592 | tf_op jit(solution)/shard_map/all_gather | solution.py:15
  310.3 3.3 multiply_reduce_fusion.1
  313.6 40.4 %psum.44 = f32[]{:T(128)} all-reduce(f32[]{:T(128)} %get-tuple-element.15), channel_id=1, replica_groups=mesh['gx'=4,'gy'=8] {'gx','gy'}, use_global_device_ids=true, to_apply=%region_6.7 | all-reduce | flops 1 | bytes 8 | tf_op jit(solution)/shard_map/psum | solution.py:48
  354.7 0.7 fusion.15
  355.5 27.4 %all-gather.39.cloned.1.call-done = bf16[2048,256]{0,1:T(8,128)(2,1)} async-done(((bf16[512,256]{0,1:T(8,128)(2,1)}), bf16[2048,256]{0,1:T(8,128)(2,1)}) %all-gather.39.cloned.1.call-update) | async-done | bytes 1048592 | tf_op jit(solution)/shard_map/all_gather | solution.py:15
  383.0 3.3 fusion.8
  386.4 0.5 all-gather.35.cloned.1.call-update
  387.0 0.7 all-gather.47.cloned.1.call-update
  387.7 0.5 all-gather.45.cloned.1.call-update
  388.2 0.2 all-gather.51.cloned.1.call-start
  388.5 25.4 %all-gather.41.cloned.1.call-done = bf16[2048,256]{1,0:T(8,128)(2,1)} async-done(((bf16[512,256]{1,0:T(8,128)(2,1)}), bf16[2048,256]{1,0:T(8,128)(2,1)}) %all-gather.41.cloned.1.call-update) | async-done | bytes 1048592 | tf_op jit(solution)/shard_map/all_gather | solution.py:15
  413.8 29.5 %all-gather.35.cloned.1.call-done = bf16[512,2048]{0,1:T(8,128)(2,1)} async-done(((bf16[512,256]{0,1:T(8,128)(2,1)}), bf16[512,2048]{0,1:T(8,128)(2,1)}) %all-gather.35.cloned.1.call-update) | async-done | bytes 2097168 | tf_op jit(solution)/shard_map/all_gather | solution.py:12
  443.3 3.3 convolution_convert_fusion.5
  446.7 26.2 %all-gather.47.cloned.1.call-done = bf16[2048,256]{1,0:T(8,128)(2,1)} async-done(((bf16[512,256]{1,0:T(8,128)(2,1)}), bf16[2048,256]{1,0:T(8,128)(2,1)}) %all-gather.47.cloned.1.call-update) | async-done | bytes 1048592 | tf_op jit(solution)/shard_map/all_gather | solution.py:15
  472.9 29.2 %all-gather.45.cloned.1.call-done = bf16[512,2048]{1,0:T(8,128)(2,1)} async-done(((bf16[512,256]{1,0:T(8,128)(2,1)}), bf16[512,2048]{1,0:T(8,128)(2,1)}) %all-gather.45.cloned.1.call-update) | async-done | bytes 2097168 | tf_op jit(solution)/shard_map/all_gather | solution.py:12
  502.2 3.3 convolution_convert_fusion.4
  505.5 0.5 all-gather.43.cloned.1.call-update
  506.1 26.2 %all-gather.51.cloned.1.call-done = bf16[2048,256]{1,0:T(8,128)(2,1)} async-done(((bf16[512,256]{1,0:T(8,128)(2,1)}), bf16[2048,256]{1,0:T(8,128)(2,1)}) %all-gather.51.cloned.1.call-update) | async-done | bytes 1048592 | tf_op jit(solution)/shard_map/all_gather | solution.py:15
  532.3 29.2 %all-gather.49.cloned.1.call-done = bf16[512,2048]{1,0:T(8,128)(2,1)} async-done(((bf16[512,256]{1,0:T(8,128)(2,1)}), bf16[512,2048]{1,0:T(8,128)(2,1)}) %all-gather.49.cloned.1.call-update) | async-done | bytes 2097168 | tf_op jit(solution)/shard_map/all_gather | solution.py:12
  561.6 3.3 fusion.9
  564.9 0.5 all-gather.59.cloned.1.call-update
  565.5 0.5 all-gather.57.cloned.1.call-update
  566.1 25.9 %all-gather.43.cloned.1.call-done = bf16[512,2048]{1,0:T(8,128)(2,1)} async-done(((bf16[512,256]{1,0:T(8,128)(2,1)}), bf16[512,2048]{1,0:T(8,128)(2,1)}) %all-gather.43.cloned.1.call-update) | async-done | bytes 2097168 | tf_op jit(solution)/shard_map/all_gather | solution.py:12
  592.0 29.4 %all-gather.53.cloned.1.call-done = bf16[2048,256]{1,0:T(8,128)(2,1)} async-done(((bf16[512,256]{1,0:T(8,128)(2,1)}), bf16[2048,256]{1,0:T(8,128)(2,1)}) %all-gather.53.cloned.1.call-update) | async-done | bytes 1048592 | tf_op jit(solution)/shard_map/all_gather | solution.py:15
  621.4 3.3 convolution_convert_fusion.3
  624.8 25.5 %all-gather.59.cloned.1.call-done = bf16[2048,256]{1,0:T(8,128)(2,1)} async-done(((bf16[512,256]{1,0:T(8,128)(2,1)}), bf16[2048,256]{1,0:T(8,128)(2,1)}) %all-gather.59.cloned.1.call-update) | async-done | bytes 1048592 | tf_op jit(solution)/shard_map/all_gather | solution.py:15
  650.2 29.2 %all-gather.57.cloned.1.call-done = bf16[512,2048]{1,0:T(8,128)(2,1)} async-done(((bf16[512,256]{1,0:T(8,128)(2,1)}), bf16[512,2048]{1,0:T(8,128)(2,1)}) %all-gather.57.cloned.1.call-update) | async-done | bytes 2097168 | tf_op jit(solution)/shard_map/all_gather | solution.py:12
  679.5 3.3 convolution_convert_fusion.2
  682.8 0.7 all-gather.55.cloned.1.call-update
  683.6 26.1 %all-gather.63.cloned.1.call-done = bf16[2048,256]{1,0:T(8,128)(2,1)} async-done(((bf16[512,256]{1,0:T(8,128)(2,1)}), bf16[2048,256]{1,0:T(8,128)(2,1)}) %all-gather.63.cloned.1.call-update) | async-done | bytes 1048592 | tf_op jit(solution)/shard_map/all_gather | solution.py:15
  709.6 29.2 %all-gather.61.cloned.1.call-done = bf16[512,2048]{1,0:T(8,128)(2,1)} async-done(((bf16[512,256]{1,0:T(8,128)(2,1)}), bf16[512,2048]{1,0:T(8,128)(2,1)}) %all-gather.61.cloned.1.call-update) | async-done | bytes 2097168 | tf_op jit(solution)/shard_map/all_gather | solution.py:12
  738.9 3.3 fusion.10
  742.2 0.7 all-gather.71.cloned.1.call-update
  743.0 0.5 all-gather.69.cloned.1.call-update
  743.5 25.9 %all-gather.55.cloned.1.call-done = bf16[512,2048]{1,0:T(8,128)(2,1)} async-done(((bf16[512,256]{1,0:T(8,128)(2,1)}), bf16[512,2048]{1,0:T(8,128)(2,1)}) %all-gather.55.cloned.1.call-update) | async-done | bytes 2097168 | tf_op jit(solution)/shard_map/all_gather | solution.py:12
  769.5 29.6 %all-gather.65.cloned.1.call-done = bf16[2048,256]{1,0:T(8,128)(2,1)} async-done(((bf16[512,256]{1,0:T(8,128)(2,1)}), bf16[2048,256]{1,0:T(8,128)(2,1)}) %all-gather.65.cloned.1.call-update) | async-done | bytes 1048592 | tf_op jit(solution)/shard_map/all_gather | solution.py:15
  799.1 3.3 convolution_convert_fusion.1
  802.4 25.6 %all-gather.71.cloned.1.call-done = bf16[2048,256]{1,0:T(8,128)(2,1)} async-done(((bf16[512,256]{1,0:T(8,128)(2,1)}), bf16[2048,256]{1,0:T(8,128)(2,1)}) %all-gather.71.cloned.1.call-update) | async-done | bytes 1048592 | tf_op jit(solution)/shard_map/all_gather | solution.py:15
  828.0 29.2 %all-gather.69.cloned.1.call-done = bf16[512,2048]{1,0:T(8,128)(2,1)} async-done(((bf16[512,256]{1,0:T(8,128)(2,1)}), bf16[512,2048]{1,0:T(8,128)(2,1)}) %all-gather.69.cloned.1.call-update) | async-done | bytes 2097168 | tf_op jit(solution)/shard_map/all_gather | solution.py:12
  857.3 3.3 convolution_convert_fusion
  860.6 0.5 all-gather.67.cloned.1.call-update
  861.2 26.2 %all-gather.75.cloned.1.call-done = bf16[2048,256]{1,0:T(8,128)(2,1)} async-done(((bf16[512,256]{1,0:T(8,128)(2,1)}), bf16[2048,256]{1,0:T(8,128)(2,1)}) %all-gather.75.cloned.1.call-update) | async-done | bytes 1048592 | tf_op jit(solution)/shard_map/all_gather | solution.py:15
  887.4 29.2 %all-gather.73.cloned.1.call-done = bf16[512,2048]{1,0:T(8,128)(2,1)} async-done(((bf16[512,256]{1,0:T(8,128)(2,1)}), bf16[512,2048]{1,0:T(8,128)(2,1)}) %all-gather.73.cloned.1.call-update) | async-done | bytes 2097168 | tf_op jit(solution)/shard_map/all_gather | solution.py:12
  916.7 3.3 fusion.11
  920.0 27.1 %all-gather.67.cloned.1.call-done = bf16[512,2048]{1,0:T(8,128)(2,1)} async-done(((bf16[512,256]{1,0:T(8,128)(2,1)}), bf16[512,2048]{1,0:T(8,128)(2,1)}) %all-gather.67.cloned.1.call-update) | async-done | bytes 2097168 | tf_op jit(solution)/shard_map/all_gather | solution.py:12
  947.1 29.6 %all-gather.77.cloned.1.call-done = bf16[2048,256]{1,0:T(8,128)(2,1)} async-done(((bf16[512,256]{1,0:T(8,128)(2,1)}), bf16[2048,256]{1,0:T(8,128)(2,1)}) %all-gather.77.cloned.1.call-update) | async-done | bytes 1048592 | tf_op jit(solution)/shard_map/all_gather | solution.py:15
  976.7 4.0 fusion.14
  980.7 40.4 %all-reduce = (f32[]{:T(128)}, f32[]{:T(128)}, f32[]{:T(128)}) all-reduce(f32[]{:T(128)} %get-tuple-element.4, f32[]{:T(128)} %get-tuple-element.12, f32[]{:T(128)} %get-tuple-element.3), channel_id=1, replica_groups=mesh['gx'=4,'gy'=8] {'gx','gy'}, use_global_device_ids=true, to_apply=%region_9.10 | all-reduce | flops 3 | bytes 24 | tf_op jit(solution)/shard_map/psum | solution.py:48
  (56 shorter events, 1.4 us)
Async XLA Ops:
  7.2 137.7 %reduce-scatter.3.cloned.1.call-start = ((), (), s32[]{:S(2)}) async-start(), calls=%async_computation.2 | async-start | bytes 18874368 | tf_op jit(solution)/shard_map/reduce_scatter | solution.py:35
  26.0 118.9 %copy-start = (f32[512,256]{1,0:T(8,128)S(1)}, f32[512,256]{1,0:T(8,128)}, u32[]{:S(2)}) copy-start(f32[512,256]{1,0:T(8,128)} %param.7) | copy-start | bytes 1572868
  26.0 169.0 %reduce-scatter.5.cloned.1.call-start = ((), (), s32[]{:S(2)}) async-start(), calls=%async_computation.3 | async-start | bytes 2621440 | tf_op jit(solution)/shard_map/reduce_scatter | solution.py:36
  144.8 75.8 %all-gather.29.cloned.1.call-start = ((), (), s32[]{:S(2)}) async-start(), calls=%async_computation.5 | async-start | bytes 1310720 | tf_op jit(solution)/shard_map/all_gather | solution.py:15
  146.3 104.1 %all-gather.27.cloned.1.call-start = ((), (), s32[]{:S(2)}) async-start(), calls=%async_computation.4 | async-start | bytes 2359296 | tf_op jit(solution)/shard_map/all_gather | solution.py:12
  146.4 46.5 %copy-start.3 = (f32[2048]{0:T(1024)S(1)}, f32[2048]{0:T(1024)}, u32[]{:S(2)}) copy-start(f32[2048]{0:T(1024)} %param.6) | copy-start | bytes 24580
  194.2 59.5 %copy-start.2 = (f32[2048]{0:T(1024)}, f32[2048]{0:T(1024)S(1)}, u32[]{:S(2)}) copy-start(f32[2048]{0:T(1024)S(1)} %get-tuple-element.11) | copy-start | bytes 24580
  196.9 83.4 %all-gather.33.cloned.1.call-start = ((), (), s32[]{:S(2)}) async-start(), calls=%async_computation.7 | async-start | bytes 2359296 | tf_op jit(solution)/shard_map/all_gather | solution.py:12
  197.5 112.8 %all-gather.31.cloned.1.call-start = ((), (), s32[]{:S(2)}) async-start(), calls=%async_computation.6 | async-start | bytes 1310720 | tf_op jit(solution)/shard_map/all_gather | solution.py:15
  253.7 101.8 %all-gather.37.cloned.1.call-start = ((), (), s32[]{:S(2)}) async-start(), calls=%async_computation.9 | async-start | bytes 2359296 | tf_op jit(solution)/shard_map/all_gather | solution.py:12
  254.7 128.3 %all-gather.39.cloned.1.call-start = ((), (), s32[]{:S(2)}) async-start(), calls=%async_computation.10 | async-start | bytes 1310720 | tf_op jit(solution)/shard_map/all_gather | solution.py:15
  355.5 58.4 %all-gather.41.cloned.1.call-start = ((), (), s32[]{:S(2)}) async-start(), calls=%async_computation.11 | async-start | bytes 1310720 | tf_op jit(solution)/shard_map/all_gather | solution.py:15
  386.3 57.0 %all-gather.35.cloned.1.call-start = ((), (), s32[]{:S(2)}) async-start(), calls=%async_computation.8 | async-start | bytes 2359296 | tf_op jit(solution)/shard_map/all_gather | solution.py:12
  386.9 86.0 %all-gather.47.cloned.1.call-start = ((), (), s32[]{:S(2)}) async-start(), calls=%async_computation.14 | async-start | bytes 1310720 | tf_op jit(solution)/shard_map/all_gather | solution.py:15
  387.7 114.5 %all-gather.45.cloned.1.call-start = ((), (), s32[]{:S(2)}) async-start(), calls=%async_computation.13 | async-start | bytes 2359296 | tf_op jit(solution)/shard_map/all_gather | solution.py:12
  388.2 144.1 %all-gather.51.cloned.1.call-start = ((), (), s32[]{:S(2)}) async-start(), calls=%async_computation.16 | async-start | bytes 1310720 | tf_op jit(solution)/shard_map/all_gather | solution.py:15
  446.7 114.9 %all-gather.49.cloned.1.call-start = ((), (), s32[]{:S(2)}) async-start(), calls=%async_computation.15 | async-start | bytes 2359296 | tf_op jit(solution)/shard_map/all_gather | solution.py:12
  505.5 86.5 %all-gather.43.cloned.1.call-start = ((), (), s32[]{:S(2)}) async-start(), calls=%async_computation.12 | async-start | bytes 2359296 | tf_op jit(solution)/shard_map/all_gather | solution.py:12
  506.1 115.4 %all-gather.53.cloned.1.call-start = ((), (), s32[]{:S(2)}) async-start(), calls=%async_computation.17 | async-start | bytes 1310720 | tf_op jit(solution)/shard_map/all_gather | solution.py:15
  564.9 85.4 %all-gather.59.cloned.1.call-start = ((), (), s32[]{:S(2)}) async-start(), calls=%async_computation.20 | async-start | bytes 1310720 | tf_op jit(solution)/shard_map/all_gather | solution.py:15
  565.5 114.0 %all-gather.57.cloned.1.call-start = ((), (), s32[]{:S(2)}) async-start(), calls=%async_computation.19 | async-start | bytes 2359296 | tf_op jit(solution)/shard_map/all_gather | solution.py:12
  566.0 143.6 %all-gather.63.cloned.1.call-start = ((), (), s32[]{:S(2)}) async-start(), calls=%async_computation.22 | async-start | bytes 1310720 | tf_op jit(solution)/shard_map/all_gather | solution.py:15
  624.7 114.1 %all-gather.61.cloned.1.call-start = ((), (), s32[]{:S(2)}) async-start(), calls=%async_computation.21 | async-start | bytes 2359296 | tf_op jit(solution)/shard_map/all_gather | solution.py:12
  682.8 86.7 %all-gather.55.cloned.1.call-start = ((), (), s32[]{:S(2)}) async-start(), calls=%async_computation.18 | async-start | bytes 2359296 | tf_op jit(solution)/shard_map/all_gather | solution.py:12
  683.5 115.5 %all-gather.65.cloned.1.call-start = ((), (), s32[]{:S(2)}) async-start(), calls=%async_computation.23 | async-start | bytes 1310720 | tf_op jit(solution)/shard_map/all_gather | solution.py:15
  742.2 85.8 %all-gather.71.cloned.1.call-start = ((), (), s32[]{:S(2)}) async-start(), calls=%async_computation.26 | async-start | bytes 1310720 | tf_op jit(solution)/shard_map/all_gather | solution.py:15
  742.9 114.3 %all-gather.69.cloned.1.call-start = ((), (), s32[]{:S(2)}) async-start(), calls=%async_computation.25 | async-start | bytes 2359296 | tf_op jit(solution)/shard_map/all_gather | solution.py:12
  743.5 143.9 %all-gather.75.cloned.1.call-start = ((), (), s32[]{:S(2)}) async-start(), calls=%async_computation.28 | async-start | bytes 1310720 | tf_op jit(solution)/shard_map/all_gather | solution.py:15
  802.3 114.3 %all-gather.73.cloned.1.call-start = ((), (), s32[]{:S(2)}) async-start(), calls=%async_computation.27 | async-start | bytes 2359296 | tf_op jit(solution)/shard_map/all_gather | solution.py:12
  860.5 86.5 %all-gather.67.cloned.1.call-start = ((), (), s32[]{:S(2)}) async-start(), calls=%async_computation.24 | async-start | bytes 2359296 | tf_op jit(solution)/shard_map/all_gather | solution.py:12
  861.1 115.5 %copy-start.1 = (f32[512,256]{1,0:T(8,128)S(1)}, f32[512,256]{1,0:T(8,128)}, u32[]{:S(2)}) copy-start(f32[512,256]{1,0:T(8,128)} %reduce-scatter.5.cloned.1.call-done) | copy-start | bytes 1572868
  861.2 115.5 %all-gather.77.cloned.1.call-start = ((), (), s32[]{:S(2)}) async-start(), calls=%async_computation.29 | async-start | bytes 1310720 | tf_op jit(solution)/shard_map/all_gather | solution.py:15
Sparse Core Ops, SparseCore 0:
  26.1 118.6 reduce-scatter.2
  147.1 44.6 reduce-scatter.4
  193.4 27.1 all-gather.28
  222.9 27.4 all-gather.26
  252.2 28.0 all-gather.32
  282.3 27.9 all-gather.30
  312.2 27.6 all-gather.36
  355.6 27.3 all-gather.38
  386.5 27.3 all-gather.40
  416.2 27.1 all-gather.34
  444.9 27.9 all-gather.46
  474.7 27.4 all-gather.44
  504.3 27.9 all-gather.50
  534.1 27.4 all-gather.48
  563.9 28.0 all-gather.42
  593.4 27.9 all-gather.52
  622.9 27.3 all-gather.58
  652.0 27.4 all-gather.56
  681.6 27.9 all-gather.62
  711.4 27.4 all-gather.60
  741.3 28.0 all-gather.54
  771.0 27.9 all-gather.64
  800.6 27.3 all-gather.70
  829.8 27.4 all-gather.68
  859.4 27.9 all-gather.74
  889.1 27.4 all-gather.72
  919.0 28.0 all-gather.66
  948.7 27.9 all-gather.76
where the time goes:
time: 1030 us
  waiting for transfers between devices  815 us (79%)
  blocking collectives  123 us (12%)
  matrix products  61.5 us (6%)
  between operations  20.3 us (2%)
  other arithmetic  10.5 us (1%)
    all_gather x13, waiting for transfers between devices, product(): lax.all_gather(right_half, 'gx', axis=0, tiled=True)  350 us
    all_gather x13, waiting for transfers between devices, product(): panel = lax.all_gather(left_half, 'gy', axis=1, tiled=True)  339 us
    reduce_scatter x1, waiting for transfers between devices, shards(): lax.psum_scatter(partial_gram, 'gy', scatter_dimension=1, tiled=True)  119 us
    psum x2, blocking collectives, shards(): lax.psum((jnp.sum(prod * prod), jnp.sum(cov_tile * identity_tile), jnp.su...  80.7 us
    dot_general x13, matrix products, product(): jnp.dot(panel, lax.all_gather(right_half, 'gx', axis=0, tiled=True), pref...  43.4 us
    psum x1, blocking collectives, shards(): total, count = lax.psum((column_total, local_count), ('gx', 'gy'))  42.2 us
  transfers between devices with their start and end apart: 28, of which 26 were waited for; matrix products, arithmetic and copies ran while one was open for 5% of the time, Pallas kernels for 0%

commit v1 on v0

--- a/solution.py
+++ b/solution.py
@@ -46,8 +46,11 @@
     half = product(cov_tile, ref_root)
     prod = product(ref_root, half)
     square_sum, cov_trace, root_square = lax.psum(
-        (jnp.sum(prod * prod), jnp.sum(cov_tile * identity_tile), jnp.sum(ref_root * ref_root)),
-        ("gx", "gy"),
+        lax.psum(
+            (jnp.sum(prod * prod), jnp.sum(cov_tile * identity_tile), jnp.sum(ref_root * ref_root)),
+            "gy",
+        ),
+        "gx",
     )
     scale = jnp.sqrt(square_sum + 1.0)
     current = prod / scale

time: 1030 us -> 1040 us (level)
    psum x0 -> x3, blocking collectives: none -> 62.7 us  [the longest x1 40.3 us: shards(): last_trace = lax.psum(jnp.sum(current * identity_tile), ('gx', 'gy'))]
    psum x2, blocking collectives: 80.7 us -> 27.2 us  [shards(): lax.psum((jnp.sum(prod * prod), jnp.sum(cov_tile * identity_tile), jnp.su...]
  transfers between devices with their start and end apart: 28 -> 28, of which waited for: 26 -> 26; matrix products, arithmetic and copies ran while one was open for 5% -> 4% of each run, Pallas kernels for 0% -> 0%
where the time goes in v1:
time: 1040 us
  waiting for transfers between devices  817 us (79%)
  blocking collectives  132 us (13%)
  matrix products  61.5 us (6%)
  between operations  20.3 us (2%)
  other arithmetic  10.4 us (1%)
    all_gather x13, waiting for transfers between devices, product(): lax.all_gather(right_half, 'gx', axis=0, tiled=True)  352 us
    all_gather x13, waiting for transfers between devices, product(): panel = lax.all_gather(left_half, 'gy', axis=1, tiled=True)  339 us
    reduce_scatter x1, waiting for transfers between devices, shards(): lax.psum_scatter(partial_gram, 'gy', scatter_dimension=1, tiled=True)  119 us
    dot_general x13, matrix products, product(): jnp.dot(panel, lax.all_gather(right_half, 'gx', axis=0, tiled=True), pref...  43.4 us
    psum x1, blocking collectives, shards(): total, count = lax.psum((column_total, local_count), ('gx', 'gy'))  42.3 us
    psum x1, blocking collectives, shards(): last_trace = lax.psum(jnp.sum(current * identity_tile), ('gx', 'gy'))  40.3 us
    psum x2, blocking collectives, shards(): lax.psum((jnp.sum(prod * prod), jnp.sum(cov_tile * identity_tile), jnp.su...  27.2 us
    psum x2, blocking collectives, shards(): lax.psum(lax.psum((jnp.sum(prod * prod), jnp.sum(cov_tile * identity_tile...  22.4 us
  transfers between devices with their start and end apart: 28, of which 26 were waited for; matrix products, arithmetic and copies ran while one was open for 4% of the time, Pallas kernels for 0%

profile of v1, /device:TPU:0, one launch (start us, length us, event | category | flops | bytes accessed | tf_op | source)
XLA Modules:
  0.0 1042.7 jit_solution(2755288852949288921)
XLA Ops:
  7.9 18.1 %fusion = f32[2048,2048]{1,0:T(8,128)} fusion(bf16[1280,2048]{1,0:T(8,128)(2,1)} %param.4, pred[1280]{0:T(1024)(128)(4,1)S(1)} %iota_compare_fusion), kind=kOutput, calls=%fused_computation.1 | convolution fusion | flops 10740039680 | bytes 22021376 | tf_op jit(solution)/shard_map/dot_general | solution.py:29
  26.1 118.8 %reduce-scatter.3.cloned.1.call-done = f32[2048,256]{1,0:T(8,128)} async-done(((f32[2048,2048]{1,0:T(8,128)}), f32[2048,256]{1,0:T(8,128)}) %reduce-scatter.3.cloned.1.call-update) | async-done | bytes 2097168 | tf_op jit(solution)/shard_map/reduce_scatter | solution.py:35
  144.9 1.3 multiply_reduce_fusion
  146.3 3.6 convert_reduce_fusion
  149.9 42.3 %all-reduce = (f32[2048]{0:T(1024)S(1)}, f32[]{:T(128)}) all-reduce(f32[2048]{0:T(1024)S(1)} %convert_reduce_fusion, f32[]{:T(128)S(6)} %convert_element_type.69), channel_id=1, replica_groups=mesh['gx'=4,'gy'=8] {'gx','gy'}, use_global_device_ids=true, to_apply=%region_1.2 | all-reduce | flops 2049 | bytes 16392 | tf_op jit(solution)/shard_map/psum | solution.py:34
  192.9 1.3 multiply_reduce_fusion.2
  194.2 0.7 dynamic-slice_multiply_fusion
  194.9 1.9 fusion.16
  196.9 0.5 all-gather.33.cloned.1.call-update
  197.5 23.1 %all-gather.29.cloned.1.call-done = bf16[2048,256]{1,0:T(8,128)(2,1)} async-done(((bf16[512,256]{1,0:T(8,128)(2,1)}), bf16[2048,256]{1,0:T(8,128)(2,1)}) %all-gather.29.cloned.1.call-update) | async-done | bytes 1048592 | tf_op jit(solution)/shard_map/all_gather | solution.py:15
  220.6 29.8 %all-gather.27.cloned.1.call-done = bf16[512,2048]{1,0:T(8,128)(2,1)} async-done(((bf16[512,256]{1,0:T(8,128)(2,1)}), bf16[512,2048]{1,0:T(8,128)(2,1)}) %all-gather.27.cloned.1.call-update) | async-done | bytes 2097168 | tf_op jit(solution)/shard_map/all_gather | solution.py:12
  250.4 3.3 convolution_convert_fusion.6
  253.8 0.8 fusion.12
  254.7 25.6 %all-gather.33.cloned.1.call-done = bf16[512,2048]{1,0:T(8,128)(2,1)} async-done(((bf16[512,256]{1,0:T(8,128)(2,1)}), bf16[512,2048]{1,0:T(8,128)(2,1)}) %all-gather.33.cloned.1.call-update) | async-done | bytes 2097168 | tf_op jit(solution)/shard_map/all_gather | solution.py:12
  280.3 30.0 %all-gather.31.cloned.1.call-done = bf16[2048,256]{1,0:T(8,128)(2,1)} async-done(((bf16[512,256]{1,0:T(8,128)(2,1)}), bf16[2048,256]{1,0:T(8,128)(2,1)}) %all-gather.31.cloned.1.call-update) | async-done | bytes 1048592 | tf_op jit(solution)/shard_map/all_gather | solution.py:15
  310.3 3.3 multiply_reduce_fusion.1
  313.6 13.8 %psum.65 = f32[]{:T(128)} all-reduce(f32[]{:T(128)} %get-tuple-element.16), channel_id=1, replica_groups=mesh['gx'=4,'gy'=8] {'gy'}, use_global_device_ids=true, to_apply=%region_6.7 | all-reduce | flops 1 | bytes 8 | tf_op jit(solution)/shard_map/psum | solution.py:49
  327.4 11.5 %psum.66 = f32[]{:T(128)} all-reduce(f32[]{:T(128)} %psum.65), channel_id=1, replica_groups=mesh['gx'=4,'gy'=8] {'gx'}, use_global_device_ids=true, to_apply=%region_7.8 | all-reduce | flops 1 | bytes 8 | tf_op jit(solution)/shard_map/psum | solution.py:48
  339.7 0.7 fusion.15
  340.5 29.4 %all-gather.39.cloned.1.call-done = bf16[2048,256]{0,1:T(8,128)(2,1)} async-done(((bf16[512,256]{0,1:T(8,128)(2,1)}), bf16[2048,256]{0,1:T(8,128)(2,1)}) %all-gather.39.cloned.1.call-update) | async-done | bytes 1048592 | tf_op jit(solution)/shard_map/all_gather | solution.py:15
  369.9 3.3 fusion.8
  373.3 0.5 all-gather.35.cloned.1.call-update
  373.9 0.7 all-gather.47.cloned.1.call-update
  374.6 0.5 all-gather.45.cloned.1.call-update
  375.2 25.6 %all-gather.41.cloned.1.call-done = bf16[2048,256]{1,0:T(8,128)(2,1)} async-done(((bf16[512,256]{1,0:T(8,128)(2,1)}), bf16[2048,256]{1,0:T(8,128)(2,1)}) %all-gather.41.cloned.1.call-update) | async-done | bytes 1048592 | tf_op jit(solution)/shard_map/all_gather | solution.py:15
  400.7 29.5 %all-gather.35.cloned.1.call-done = bf16[512,2048]{0,1:T(8,128)(2,1)} async-done(((bf16[512,256]{0,1:T(8,128)(2,1)}), bf16[512,2048]{0,1:T(8,128)(2,1)}) %all-gather.35.cloned.1.call-update) | async-done | bytes 2097168 | tf_op jit(solution)/shard_map/all_gather | solution.py:12
  430.2 3.3 convolution_convert_fusion.5
  433.8 26.0 %all-gather.47.cloned.1.call-done = bf16[2048,256]{1,0:T(8,128)(2,1)} async-done(((bf16[512,256]{1,0:T(8,128)(2,1)}), bf16[2048,256]{1,0:T(8,128)(2,1)}) %all-gather.47.cloned.1.call-update) | async-done | bytes 1048592 | tf_op jit(solution)/shard_map/all_gather | solution.py:15
  459.8 29.2 %all-gather.45.cloned.1.call-done = bf16[512,2048]{1,0:T(8,128)(2,1)} async-done(((bf16[512,256]{1,0:T(8,128)(2,1)}), bf16[512,2048]{1,0:T(8,128)(2,1)}) %all-gather.45.cloned.1.call-update) | async-done | bytes 2097168 | tf_op jit(solution)/shard_map/all_gather | solution.py:12
  489.1 3.3 convolution_convert_fusion.4
  492.4 0.5 all-gather.43.cloned.1.call-update
  493.0 26.2 %all-gather.51.cloned.1.call-done = bf16[2048,256]{1,0:T(8,128)(2,1)} async-done(((bf16[512,256]{1,0:T(8,128)(2,1)}), bf16[2048,256]{1,0:T(8,128)(2,1)}) %all-gather.51.cloned.1.call-update) | async-done | bytes 1048592 | tf_op jit(solution)/shard_map/all_gather | solution.py:15
  519.2 29.2 %all-gather.49.cloned.1.call-done = bf16[512,2048]{1,0:T(8,128)(2,1)} async-done(((bf16[512,256]{1,0:T(8,128)(2,1)}), bf16[512,2048]{1,0:T(8,128)(2,1)}) %all-gather.49.cloned.1.call-update) | async-done | bytes 2097168 | tf_op jit(solution)/shard_map/all_gather | solution.py:12
  548.5 3.3 fusion.9
  551.8 0.5 all-gather.59.cloned.1.call-update
  552.4 0.5 all-gather.57.cloned.1.call-update
  553.0 25.9 %all-gather.43.cloned.1.call-done = bf16[512,2048]{1,0:T(8,128)(2,1)} async-done(((bf16[512,256]{1,0:T(8,128)(2,1)}), bf16[512,2048]{1,0:T(8,128)(2,1)}) %all-gather.43.cloned.1.call-update) | async-done | bytes 2097168 | tf_op jit(solution)/shard_map/all_gather | solution.py:12
  578.9 29.4 %all-gather.53.cloned.1.call-done = bf16[2048,256]{1,0:T(8,128)(2,1)} async-done(((bf16[512,256]{1,0:T(8,128)(2,1)}), bf16[2048,256]{1,0:T(8,128)(2,1)}) %all-gather.53.cloned.1.call-update) | async-done | bytes 1048592 | tf_op jit(solution)/shard_map/all_gather | solution.py:15
  608.3 3.3 convolution_convert_fusion.3
  611.7 25.5 %all-gather.59.cloned.1.call-done = bf16[2048,256]{1,0:T(8,128)(2,1)} async-done(((bf16[512,256]{1,0:T(8,128)(2,1)}), bf16[2048,256]{1,0:T(8,128)(2,1)}) %all-gather.59.cloned.1.call-update) | async-done | bytes 1048592 | tf_op jit(solution)/shard_map/all_gather | solution.py:15
  637.1 29.2 %all-gather.57.cloned.1.call-done = bf16[512,2048]{1,0:T(8,128)(2,1)} async-done(((bf16[512,256]{1,0:T(8,128)(2,1)}), bf16[512,2048]{1,0:T(8,128)(2,1)}) %all-gather.57.cloned.1.call-update) | async-done | bytes 2097168 | tf_op jit(solution)/shard_map/all_gather | solution.py:12
  666.4 3.3 convolution_convert_fusion.2
  669.7 0.7 all-gather.55.cloned.1.call-update
  670.5 26.1 %all-gather.63.cloned.1.call-done = bf16[2048,256]{1,0:T(8,128)(2,1)} async-done(((bf16[512,256]{1,0:T(8,128)(2,1)}), bf16[2048,256]{1,0:T(8,128)(2,1)}) %all-gather.63.cloned.1.call-update) | async-done | bytes 1048592 | tf_op jit(solution)/shard_map/all_gather | solution.py:15
  696.5 29.2 %all-gather.61.cloned.1.call-done = bf16[512,2048]{1,0:T(8,128)(2,1)} async-done(((bf16[512,256]{1,0:T(8,128)(2,1)}), bf16[512,2048]{1,0:T(8,128)(2,1)}) %all-gather.61.cloned.1.call-update) | async-done | bytes 2097168 | tf_op jit(solution)/shard_map/all_gather | solution.py:12
  725.8 3.3 fusion.10
  729.1 0.7 all-gather.71.cloned.1.call-update
  729.9 0.5 all-gather.69.cloned.1.call-update
  730.4 25.9 %all-gather.55.cloned.1.call-done = bf16[512,2048]{1,0:T(8,128)(2,1)} async-done(((bf16[512,256]{1,0:T(8,128)(2,1)}), bf16[512,2048]{1,0:T(8,128)(2,1)}) %all-gather.55.cloned.1.call-update) | async-done | bytes 2097168 | tf_op jit(solution)/shard_map/all_gather | solution.py:12
  756.4 29.6 %all-gather.65.cloned.1.call-done = bf16[2048,256]{1,0:T(8,128)(2,1)} async-done(((bf16[512,256]{1,0:T(8,128)(2,1)}), bf16[2048,256]{1,0:T(8,128)(2,1)}) %all-gather.65.cloned.1.call-update) | async-done | bytes 1048592 | tf_op jit(solution)/shard_map/all_gather | solution.py:15
  786.0 3.3 convolution_convert_fusion.1
  789.3 25.6 %all-gather.71.cloned.1.call-done = bf16[2048,256]{1,0:T(8,128)(2,1)} async-done(((bf16[512,256]{1,0:T(8,128)(2,1)}), bf16[2048,256]{1,0:T(8,128)(2,1)}) %all-gather.71.cloned.1.call-update) | async-done | bytes 1048592 | tf_op jit(solution)/shard_map/all_gather | solution.py:15
  814.9 29.2 %all-gather.69.cloned.1.call-done = bf16[512,2048]{1,0:T(8,128)(2,1)} async-done(((bf16[512,256]{1,0:T(8,128)(2,1)}), bf16[512,2048]{1,0:T(8,128)(2,1)}) %all-gather.69.cloned.1.call-update) | async-done | bytes 2097168 | tf_op jit(solution)/shard_map/all_gather | solution.py:12
  844.2 3.3 convolution_convert_fusion
  847.5 0.5 all-gather.67.cloned.1.call-update
  848.1 26.2 %all-gather.75.cloned.1.call-done = bf16[2048,256]{1,0:T(8,128)(2,1)} async-done(((bf16[512,256]{1,0:T(8,128)(2,1)}), bf16[2048,256]{1,0:T(8,128)(2,1)}) %all-gather.75.cloned.1.call-update) | async-done | bytes 1048592 | tf_op jit(solution)/shard_map/all_gather | solution.py:15
  874.3 29.2 %all-gather.73.cloned.1.call-done = bf16[512,2048]{1,0:T(8,128)(2,1)} async-done(((bf16[512,256]{1,0:T(8,128)(2,1)}), bf16[512,2048]{1,0:T(8,128)(2,1)}) %all-gather.73.cloned.1.call-update) | async-done | bytes 2097168 | tf_op jit(solution)/shard_map/all_gather | solution.py:12
  903.6 3.3 fusion.11
  906.9 27.1 %all-gather.67.cloned.1.call-done = bf16[512,2048]{1,0:T(8,128)(2,1)} async-done(((bf16[512,256]{1,0:T(8,128)(2,1)}), bf16[512,2048]{1,0:T(8,128)(2,1)}) %all-gather.67.cloned.1.call-update) | async-done | bytes 2097168 | tf_op jit(solution)/shard_map/all_gather | solution.py:12
  934.0 29.6 %all-gather.77.cloned.1.call-done = bf16[2048,256]{1,0:T(8,128)(2,1)} async-done(((bf16[512,256]{1,0:T(8,128)(2,1)}), bf16[2048,256]{1,0:T(8,128)(2,1)}) %all-gather.77.cloned.1.call-update) | async-done | bytes 1048592 | tf_op jit(solution)/shard_map/all_gather | solution.py:15
  963.6 4.0 fusion.14
  967.6 40.3 %psum.71 = f32[]{:T(128)} all-reduce(f32[]{:T(128)} %get-tuple-element.3), channel_id=1, replica_groups=mesh['gx'=4,'gy'=8] {'gx','gy'}, use_global_device_ids=true, to_apply=%region_16.17 | all-reduce | flops 1 | bytes 8 | tf_op jit(solution)/shard_map/psum | solution.py:61
  1008.5 13.4 %all-reduce.1 = (f32[]{:T(128)}, f32[]{:T(128)}) all-reduce(f32[]{:T(128)} %get-tuple-element.4, f32[]{:T(128)} %get-tuple-element.13), channel_id=1, replica_groups=mesh['gx'=4,'gy'=8] {'gy'}, use_global_device_ids=true, to_apply=%region_10.11 | all-reduce | flops 2 | bytes 16 | tf_op jit(solution)/shard_map/psum | solution.py:49
  1021.9 10.9 %all-reduce.2 = (f32[]{:T(128)}, f32[]{:T(128)}) all-reduce(f32[]{:T(128)} %get-tuple-element.7, f32[]{:T(128)} %get-tuple-element.8), channel_id=1, replica_groups=mesh['gx'=4,'gy'=8] {'gx'}, use_global_device_ids=true, to_apply=%region_11.12 | all-reduce | flops 2 | bytes 16 | tf_op jit(solution)/shard_map/psum | solution.py:48
  (59 shorter events, 1.7 us)
Async XLA Ops:
  7.2 137.7 %reduce-scatter.3.cloned.1.call-start = ((), (), s32[]{:S(2)}) async-start(), calls=%async_computation.2 | async-start | bytes 18874368 | tf_op jit(solution)/shard_map/reduce_scatter | solution.py:35
  26.0 118.9 %copy-start = (f32[512,256]{1,0:T(8,128)S(1)}, f32[512,256]{1,0:T(8,128)}, u32[]{:S(2)}) copy-start(f32[512,256]{1,0:T(8,128)} %param.7) | copy-start | bytes 1572868
  26.0 168.9 %reduce-scatter.5.cloned.1.call-start = ((), (), s32[]{:S(2)}) async-start(), calls=%async_computation.3 | async-start | bytes 2621440 | tf_op jit(solution)/shard_map/reduce_scatter | solution.py:36
  144.8 75.8 %all-gather.29.cloned.1.call-start = ((), (), s32[]{:S(2)}) async-start(), calls=%async_computation.5 | async-start | bytes 1310720 | tf_op jit(solution)/shard_map/all_gather | solution.py:15
  146.3 104.2 %all-gather.27.cloned.1.call-start = ((), (), s32[]{:S(2)}) async-start(), calls=%async_computation.4 | async-start | bytes 2359296 | tf_op jit(solution)/shard_map/all_gather | solution.py:12
  146.3 46.6 %copy-start.3 = (f32[2048]{0:T(1024)S(1)}, f32[2048]{0:T(1024)}, u32[]{:S(2)}) copy-start(f32[2048]{0:T(1024)} %param.6) | copy-start | bytes 24580
  194.1 59.6 %copy-start.2 = (f32[2048]{0:T(1024)}, f32[2048]{0:T(1024)S(1)}, u32[]{:S(2)}) copy-start(f32[2048]{0:T(1024)S(1)} %get-tuple-element.12) | copy-start | bytes 24580
  196.8 83.5 %all-gather.33.cloned.1.call-start = ((), (), s32[]{:S(2)}) async-start(), calls=%async_computation.7 | async-start | bytes 2359296 | tf_op jit(solution)/shard_map/all_gather | solution.py:12
  197.4 112.9 %all-gather.31.cloned.1.call-start = ((), (), s32[]{:S(2)}) async-start(), calls=%async_computation.6 | async-start | bytes 1310720 | tf_op jit(solution)/shard_map/all_gather | solution.py:15
  253.7 86.8 %all-gather.37.cloned.1.call-start = ((), (), s32[]{:S(2)}) async-start(), calls=%async_computation.9 | async-start | bytes 2359296 | tf_op jit(solution)/shard_map/all_gather | solution.py:12
  254.7 115.2 %all-gather.39.cloned.1.call-start = ((), (), s32[]{:S(2)}) async-start(), calls=%async_computation.10 | async-start | bytes 1310720 | tf_op jit(solution)/shard_map/all_gather | solution.py:15
  340.4 60.3 %all-gather.41.cloned.1.call-start = ((), (), s32[]{:S(2)}) async-start(), calls=%async_computation.11 | async-start | bytes 1310720 | tf_op jit(solution)/shard_map/all_gather | solution.py:15
  373.2 57.0 %all-gather.35.cloned.1.call-start = ((), (), s32[]{:S(2)}) async-start(), calls=%async_computation.8 | async-start | bytes 2359296 | tf_op jit(solution)/shard_map/all_gather | solution.py:12
  373.8 86.0 %all-gather.47.cloned.1.call-start = ((), (), s32[]{:S(2)}) async-start(), calls=%async_computation.14 | async-start | bytes 1310720 | tf_op jit(solution)/shard_map/all_gather | solution.py:15
  374.6 114.5 %all-gather.45.cloned.1.call-start = ((), (), s32[]{:S(2)}) async-start(), calls=%async_computation.13 | async-start | bytes 2359296 | tf_op jit(solution)/shard_map/all_gather | solution.py:12
  375.1 144.1 %all-gather.51.cloned.1.call-start = ((), (), s32[]{:S(2)}) async-start(), calls=%async_computation.16 | async-start | bytes 1310720 | tf_op jit(solution)/shard_map/all_gather | solution.py:15
  433.6 114.9 %all-gather.49.cloned.1.call-start = ((), (), s32[]{:S(2)}) async-start(), calls=%async_computation.15 | async-start | bytes 2359296 | tf_op jit(solution)/shard_map/all_gather | solution.py:12
  492.4 86.5 %all-gather.43.cloned.1.call-start = ((), (), s32[]{:S(2)}) async-start(), calls=%async_computation.12 | async-start | bytes 2359296 | tf_op jit(solution)/shard_map/all_gather | solution.py:12
  492.9 115.4 %all-gather.53.cloned.1.call-start = ((), (), s32[]{:S(2)}) async-start(), calls=%async_computation.17 | async-start | bytes 1310720 | tf_op jit(solution)/shard_map/all_gather | solution.py:15
  551.8 85.4 %all-gather.59.cloned.1.call-start = ((), (), s32[]{:S(2)}) async-start(), calls=%async_computation.20 | async-start | bytes 1310720 | tf_op jit(solution)/shard_map/all_gather | solution.py:15
  552.4 114.0 %all-gather.57.cloned.1.call-start = ((), (), s32[]{:S(2)}) async-start(), calls=%async_computation.19 | async-start | bytes 2359296 | tf_op jit(solution)/shard_map/all_gather | solution.py:12
  552.9 143.6 %all-gather.63.cloned.1.call-start = ((), (), s32[]{:S(2)}) async-start(), calls=%async_computation.22 | async-start | bytes 1310720 | tf_op jit(solution)/shard_map/all_gather | solution.py:15
  611.6 114.1 %all-gather.61.cloned.1.call-start = ((), (), s32[]{:S(2)}) async-start(), calls=%async_computation.21 | async-start | bytes 2359296 | tf_op jit(solution)/shard_map/all_gather | solution.py:12
  669.7 86.7 %all-gather.55.cloned.1.call-start = ((), (), s32[]{:S(2)}) async-start(), calls=%async_computation.18 | async-start | bytes 2359296 | tf_op jit(solution)/shard_map/all_gather | solution.py:12
  670.4 115.5 %all-gather.65.cloned.1.call-start = ((), (), s32[]{:S(2)}) async-start(), calls=%async_computation.23 | async-start | bytes 1310720 | tf_op jit(solution)/shard_map/all_gather | solution.py:15
  729.1 85.8 %all-gather.71.cloned.1.call-start = ((), (), s32[]{:S(2)}) async-start(), calls=%async_computation.26 | async-start | bytes 1310720 | tf_op jit(solution)/shard_map/all_gather | solution.py:15
  729.8 114.3 %all-gather.69.cloned.1.call-start = ((), (), s32[]{:S(2)}) async-start(), calls=%async_computation.25 | async-start | bytes 2359296 | tf_op jit(solution)/shard_map/all_gather | solution.py:12
  730.4 143.9 %all-gather.75.cloned.1.call-start = ((), (), s32[]{:S(2)}) async-start(), calls=%async_computation.28 | async-start | bytes 1310720 | tf_op jit(solution)/shard_map/all_gather | solution.py:15
  789.2 114.3 %all-gather.73.cloned.1.call-start = ((), (), s32[]{:S(2)}) async-start(), calls=%async_computation.27 | async-start | bytes 2359296 | tf_op jit(solution)/shard_map/all_gather | solution.py:12
  847.4 86.5 %all-gather.67.cloned.1.call-start = ((), (), s32[]{:S(2)}) async-start(), calls=%async_computation.24 | async-start | bytes 2359296 | tf_op jit(solution)/shard_map/all_gather | solution.py:12
  848.0 115.5 %copy-start.1 = (f32[512,256]{1,0:T(8,128)S(1)}, f32[512,256]{1,0:T(8,128)}, u32[]{:S(2)}) copy-start(f32[512,256]{1,0:T(8,128)} %reduce-scatter.5.cloned.1.call-done) | copy-start | bytes 1572868
  848.0 115.5 %all-gather.77.cloned.1.call-start = ((), (), s32[]{:S(2)}) async-start(), calls=%async_computation.29 | async-start | bytes 1310720 | tf_op jit(solution)/shard_map/all_gather | solution.py:15
Sparse Core Ops, SparseCore 0:
  26.1 118.6 reduce-scatter.2
  147.1 44.6 reduce-scatter.4
  193.4 27.1 all-gather.28
  222.9 27.4 all-gather.26
  252.2 28.0 all-gather.32
  282.3 27.9 all-gather.30
  312.2 27.5 all-gather.36
  341.9 27.9 all-gather.38
  373.4 27.3 all-gather.40
  403.1 27.1 all-gather.34
  431.8 27.9 all-gather.46
  461.6 27.4 all-gather.44
  491.2 27.9 all-gather.50
  521.0 27.4 all-gather.48
  550.8 28.0 all-gather.42
  580.3 27.9 all-gather.52
  609.8 27.3 all-gather.58
  638.9 27.4 all-gather.56
  668.5 27.9 all-gather.62
  698.3 27.4 all-gather.60
  728.2 28.0 all-gather.54
  757.9 27.9 all-gather.64
  787.5 27.3 all-gather.70
  816.6 27.4 all-gather.68
  846.3 27.9 all-gather.74
  876.0 27.4 all-gather.72
  905.9 28.0 all-gather.66
  935.6 27.9 all-gather.76
